TPU v7x, 32 devices: a whole 2x2x4 slice. The times are simulated.
32 devices in a mesh: groups: 2 (over x), seq: 16 (over z, y, core).
Axes of the slice: x: 2, y: 2, z: 4, core: 2. Of those that a mesh axis runs over, the one named last changes fastest.
Arguments:
- queries: bfloat16 [64, 128, 576], P('groups', 'seq'), parts along dimension 0, may hold values from -8 to 8
- prefix_pool: bfloat16 [1024, 64, 576], P(('groups', 'seq')), parts along dimension 0, may hold values from -6 to 6
- block_table: int32 [8, 128], P('groups'), parts along dimension 0, may hold values from 0 to 511, as said below
- prefix_of: int32 [64], P('groups'), parts along dimension 0, may hold values from 0 to 3
- suffix_cache: bfloat16 [64, 2048, 576], P('groups', 'seq'), parts along dimension 0, may hold values from -24 to 24
- suffix_len: int32 [64], P('groups'), parts along dimension 0, may hold values from 2 to 2048
Outputs:
- context: bfloat16 [64, 128, 512], P('groups', 'seq'), parts along dimension 0
There are 2 independent parts, one for each index of `groups`. A program takes and returns all parts, laid end to end along the dimension named above; each array names one. Nothing has to cross between parts.
Inputs may be any that keep to these rules, and one draw needn't show every extreme that they name: `block_table`: each of the 512 pool blocks is named exactly once in the table, and of each aligned run of 32 pool blocks exactly 8 belong to each prefix.
All inputs are finite; a program needn't handle non-finite values.
Results may differ from a plain program's by a relative error of at most 0.0033.
Values may be sent and summed in bfloat16 or wider, within the bound.
A program may use at most 128 MiB of HBM per device.

v0:
```python
import jax
import jax.numpy as jnp
from jax import lax
from jax.sharding import PartitionSpec as P

LAT = 512
score_scale = 192.0 ** (-0.5)


def body(queries, prefix_pool, block_table, prefix_of, suffix_cache, suffix_len):
    blocks_here, block_rows, channels = prefix_pool.shape
    prefix_total = block_table.shape[0]
    slots_here = suffix_cache.shape[1]
    position = lax.axis_index("seq")
    block_ids = position * blocks_here + lax.iota(jnp.int32, blocks_here)
    owners = jnp.any(block_table[:, :, None] == block_ids[None, None, :], axis=1)
    prefix_ids = lax.iota(jnp.int32, prefix_total)
    labels = jnp.sum(owners.astype(jnp.int32) * prefix_ids[:, None], axis=0)
    order = jnp.argsort(labels, stable=True)
    segment_rows = blocks_here // prefix_total * block_rows
    segments = prefix_pool[order].reshape(prefix_total, segment_rows, channels)
    request_keys = jnp.concatenate([segments[prefix_of], suffix_cache], axis=1)
    slot_ids = position * slots_here + lax.iota(jnp.int32, slots_here)
    live_slots = slot_ids[None, :] < suffix_len[:, None]
    visible = jnp.concatenate(
        [jnp.ones((live_slots.shape[0], segment_rows), bool), live_slots], axis=1
    )
    scores = (
        jnp.einsum(
            "rhw,rkw->rhk",
            lax.all_gather(queries, "seq", axis=1, tiled=True),
            request_keys,
            preferred_element_type=jnp.float32,
        )
        * score_scale
    )
    scores = jnp.where(visible[:, None, :], scores, -jnp.inf)
    highest = lax.pmax(jnp.max(scores, axis=2), "seq")
    weights = jnp.exp(scores - highest[:, :, None])
    weight_sum = jnp.sum(weights, axis=2)
    rounded = weights.astype(jnp.bfloat16)
    weighted = jnp.einsum(
        "rhk,rkl->rhl", rounded, request_keys[:, :, :LAT], preferred_element_type=jnp.float32
    )
    weight_sum, weighted = (
        lax.psum_scatter(weight_sum, "seq", scatter_dimension=1, tiled=True),
        lax.psum_scatter(weighted, "seq", scatter_dimension=1, tiled=True),
    )
    return (weighted / weight_sum[:, :, None]).astype(jnp.bfloat16)


def solution(mesh):
    return jax.shard_map(
        body,
        mesh=mesh,
        in_specs=(
            P("groups", "seq", None),
            P(("groups", "seq"), None, None),
            P("groups", None),
            P("groups"),
            P("groups", "seq", None),
            P("groups"),
        ),
        out_specs=P("groups", "seq", None),
        check_vma=False,
    )
```

profile of v0, /device:TPU:0, one launch (start us, length us, event | category | flops | bytes accessed | tf_op | source)
XLA Modules:
  0.0 271.6 jit_solution(3408118859675830077)
XLA Ops:
  6.5 0.0 copy-start
  6.5 0.0 all-gather.2.cloned.1.call-start
  6.5 0.7 all-gather.2.cloned.1.call-update
  7.3 0.0 reduce-scatter.3.cloned.1.call-start
  7.3 0.9 compare_reduce_fusion
  8.2 1.6 sort.17
  9.9 0.7 compare_select_fusion
  10.5 0.0 copy-done
  10.5 2.4 gather_fusion
  12.9 2.9 %copy.17 = bf16[4,512,576]{1,2,0:T(8,128)(2,1)S(1)} copy(bf16[4,512,576]{2,1,0:T(8,128)(2,1)} %bitcast.16) | data formatting | bytes 4718592 | tf_op jit(solution)/shard_map/reshape | solution.py:21
  15.8 0.0 copy-start.2
  15.9 8.0 %gather_fusion.1 = bf16[32,512,576]{1,2,0:T(8,128)(2,1)} fusion(bf16[4,512,576]{1,2,0:T(8,128)(2,1)S(1)} %copy.17, s32[1024]{0:T(1024)S(1)} %get-tuple-element.9), kind=kCustom, calls=%fused_computation.1 | custom fusion | bytes 37748864 | tf_op jit(solution)/shard_map/gather | solution.py:22
  23.8 0.0 copy-done.2
  23.8 0.1 broadcast_compare_fusion
  23.9 16.9 %constant_dynamic-update-slice_fusion.1 = bf16[32,640,576]{1,2,0:T(8,128)(2,1)} fusion(bf16[32,512,576]{1,2,0:T(8,128)(2,1)} %gather_fusion.1), kind=kLoop, calls=%fused_computation.20 | loop fusion | bytes 37748736
  40.8 5.0 %constant_dynamic-update-slice_fusion = bf16[32,640,576]{1,2,0:T(8,128)(2,1)} fusion(bf16[32,640,576]{1,2,0:T(8,128)(2,1)} %constant_dynamic-update-slice_fusion.1, bf16[32,128,576]{1,2,0:T(8,128)(2,1)} %param.10), kind=kLoop, calls=%fused_computation.19 | loop fusion | bytes 9437184 | tf_op jit(solution)/shard_map/concatenate | solution.py:22
  45.8 22.8 %all-gather.2.cloned.1.call-done = bf16[32,128,576]{2,1,0:T(8,128)(2,1)} async-done(((bf16[32,8,576]{2,1,0:T(8,128)(2,1)}), bf16[32,128,576]{2,1,0:T(8,128)(2,1)}) %all-gather.2.cloned.1.call-update) | async-done | bytes 4718608 | tf_op jit(solution)/shard_map/all_gather | solution.py:31
  68.5 17.1 %bitcast_reduce_fusion = (f32[32,128]{1,0:T(8,128)S(1)}, f32[32,640,128]{2,1,0:T(8,128)}) fusion(pred[32,640]{1,0:T(8,128)(4,1)S(1)} %concatenate.6, bf16[32,640,576]{1,2,0:T(8,128)(2,1)} %constant_dynamic-update-slice_fusion, bf16[32,128,576]{2,1,0:T(8,128)(2,1)} %all-gather.2.cloned.1.call-done), kind=kOutput, calls=%fused_computation.5 | convolution fusion | flops 3027759104 | bytes 38834176 | tf_op jit(solution)/shard_map/rhw,rkw->rhk/dot_general | solution.py:29
  85.6 59.2 %pmax.7 = f32[32,128]{1,0:T(8,128)S(1)} all-reduce(f32[32,128]{1,0:T(8,128)S(1)} %get-tuple-element.7), channel_id=1, replica_groups=mesh['groups'=2,'seq'=16] {'seq'}, use_global_device_ids=true, to_apply=%region_4.5 | all-reduce | flops 4096 | bytes 32768 | tf_op jit(solution)/shard_map/pmax | solution.py:38
  144.8 0.0 copy-start.3
  144.8 0.0 copy-start.1
  144.8 16.3 %fusion = f32[32,128,512]{2,1,0:T(8,128)} fusion(bf16[32,640,576]{1,2,0:T(8,128)(2,1)} %constant_dynamic-update-slice_fusion, f32[32,640,128]{2,1,0:T(8,128)} %get-tuple-element.8, f32[32,128]{1,0:T(8,128)S(1)} %pmax.7, pred[32,640]{1,0:T(8,128)(4,1)S(1)} %concatenate.6), kind=kOutput, calls=%fused_computation.2 | convolution fusion | flops 2694840320 | bytes 39882752 | tf_op jit(solution)/shard_map/rhk,rkl->rhl/dot_general | solution.py:42
  161.1 0.0 reduce-scatter.3.cloned.1.call-update
  161.1 0.0 copy-done.3
  161.1 0.6 dynamic-slice
  162.3 9.0 %fusion.3 = f32[32,128]{1,0:T(8,128)S(1)} fusion(f32[32,640,128]{2,1,0:T(8,128)} %get-tuple-element.8, f32[32,128]{1,0:T(8,128)S(1)} %pmax.7, pred[32,640]{1,0:T(8,128)(4,1)S(1)} %concatenate.6), kind=kLoop, calls=%fused_computation.8 | loop fusion | flops 10481664 | bytes 10539008 | tf_op jit(solution)/shard_map/reduce_sum | solution.py:40
  171.4 60.6 %all-reduce.1 = f32[32,128]{1,0:T(8,128)S(1)} all-reduce(f32[32,128]{1,0:T(8,128)S(1)} %fusion.3), channel_id=3, replica_groups=mesh['groups'=2,'seq'=16] {'seq'}, use_global_device_ids=true, to_apply=%region_7.8.clone | all-reduce | flops 4096 | bytes 32768
  231.9 0.1 constant_dynamic-slice_fusion
  232.0 30.9 %reduce-scatter.3.cloned.1.call-done = f32[32,8,512]{2,1,0:T(8,128)} async-done(((f32[32,128,512]{2,1,0:T(8,128)}), f32[32,8,512]{2,1,0:T(8,128)}) %reduce-scatter.3.cloned.1.call-update) | async-done | bytes 524304 | tf_op jit(solution)/shard_map/reduce_scatter | solution.py:47
  262.9 1.9 divide_convert_fusion
  264.8 0.0 copy-done.1
  (7 shorter events, 0.1 us)
Async XLA Ops:
  6.5 4.0 %copy-start = (bf16[32,64,576]{2,1,0:T(8,128)(2,1)S(1)}, bf16[32,64,576]{2,1,0:T(8,128)(2,1)}, u32[]{:S(2)}) copy-start(bf16[32,64,576]{2,1,0:T(8,128)(2,1)} %param.7) | copy-start | bytes 7077892
  6.5 62.0 %all-gather.2.cloned.1.call-start = ((), (), s32[]{:S(2)}) async-start(), calls=%async_computation.1 | async-start | bytes 5570560 | tf_op jit(solution)/shard_map/all_gather | solution.py:31
  7.3 255.7 %reduce-scatter.3.cloned.1.call-start = ((), (), s32[]{:S(2)}) async-start(), calls=%async_computation.2 | async-start | bytes 8912896 | tf_op jit(solution)/shard_map/reduce_scatter | solution.py:47
  15.8 8.0 %copy-start.2 = (s32[32]{0:T(128)S(1)}, s32[32]{0:T(128)}, u32[]{:S(2)}) copy-start(s32[32]{0:T(128)} %param.11) | copy-start | bytes 388
  144.8 16.3 %copy-start.3 = (u32[32]{0:T(128)S(1)}, u32[32]{0:T(128)}, u32[]{:S(2)}) copy-start(u32[32]{0:T(128)} %constant.30) | copy-start | bytes 388
  144.8 120.0 %copy-start.1 = (bf16[32,64,576]{2,1,0:T(8,128)(2,1)S(1)}, bf16[32,64,576]{2,1,0:T(8,128)(2,1)}, u32[]{:S(2)}) copy-start(bf16[32,64,576]{2,1,0:T(8,128)(2,1)} %param.7) | copy-start | bytes 7077892
Sparse Core Ops, SparseCore 0:
  9.5 58.9 all-gather.1
  161.2 101.6 reduce-scatter.2
where the time goes:
time: 272 us
  blocking collectives  120 us (44%)
  waiting for transfers between devices  54.4 us (20%)
  local copies, waits for them, and re-layouts  35.8 us (13%)
  matrix products  33.4 us (12%)
  other arithmetic  14.1 us (5%)
  between operations  14.1 us (5%)
    unnamed x1, blocking collectives  60.6 us
    pmax x1, blocking collectives, body(): highest = lax.pmax(jnp.max(scores, axis=2), 'seq')  59.2 us
    reduce_scatter x1, waiting for transfers between devices, body(): lax.psum_scatter(weighted, 'seq', scatter_dimension=1, tiled=True)  30.9 us
    all_gather x1, waiting for transfers between devices, body(): lax.all_gather(queries, 'seq', axis=1, tiled=True)  22.8 us
    unnamed x11, local copies, waits for them, and re-layouts  17.6 us
    dot_general x1, matrix products, body(): jnp.einsum('rhw,rkw->rhk', lax.all_gather(queries, 'seq', axis=1, tiled=T...  17.1 us
    dot_general x1, matrix products, body(): jnp.einsum('rhk,rkl->rhl', rounded, request_keys[:, :, :LAT], preferred_e...  16.3 us
    reduce_sum x1, other arithmetic, body(): weight_sum = jnp.sum(weights, axis=2)  9.02 us
  transfers between devices with their start and end apart: 2, of which 2 were waited for; matrix products, arithmetic and copies ran while one was open for 18% of the time, Pallas kernels for 0%

commit v1 on v0

--- a/solution.py
+++ b/solution.py
@@ -5,6 +5,31 @@
 
 LAT = 512
 score_scale = 192.0 ** (-0.5)
+
+
+def joined_along(blocks, dim):
+    lengths = list(blocks.shape[1:])
+    lengths[dim] *= blocks.shape[0]
+    return jnp.moveaxis(blocks, 0, dim).reshape(lengths)
+
+
+def ring_apply(x, axis, dim, apply, out_dim):
+    size, index, extent = (lax.axis_size(axis), lax.axis_index(axis), x.shape[dim])
+    ahead = [(i, (i + 1) % size) for i in range(size)]
+    backward = [(i, (i - 1) % size) for i in range(size)]
+    middle = size // 2
+    tiles = {}
+    from_left = from_right = x
+    for hop in range(middle + 1):
+        next_left = lax.ppermute(from_left, axis, ahead) if hop < middle else None
+        next_right = lax.ppermute(from_right, axis, backward) if hop < size - middle - 1 else None
+        tiles[-hop] = apply(from_left, (index - hop) % size * extent)
+        if 0 < hop < size - middle:
+            tiles[hop] = apply(from_right, (index + hop) % size * extent)
+        from_left, from_right = (next_left, next_right)
+    tiles = jnp.stack([tiles[k] for k in sorted(tiles)])
+    tiles = tiles[(jnp.arange(size) - index + middle) % size]
+    return joined_along(tiles, out_dim)
 
 
 def body(queries, prefix_pool, block_table, prefix_of, suffix_cache, suffix_len):
@@ -26,11 +51,14 @@
         [jnp.ones((live_slots.shape[0], segment_rows), bool), live_slots], axis=1
     )
     scores = (
-        jnp.einsum(
-            "rhw,rkw->rhk",
-            lax.all_gather(queries, "seq", axis=1, tiled=True),
-            request_keys,
-            preferred_element_type=jnp.float32,
+        ring_apply(
+            queries,
+            "seq",
+            1,
+            lambda shard, start: jnp.einsum(
+                "rhw,rkw->rhk", shard, request_keys, preferred_element_type=jnp.float32
+            ),
+            1,
         )
         * score_scale
     )

time: 272 us -> 470 us (1.73)
  matrix products: 33.4 us -> 181 us
  starting transfers between devices: 0.04 us -> 32 us
  local copies, waits for them, and re-layouts: 35.8 us -> 46 us
  other arithmetic: 14.1 us -> 21.3 us
    dot_general x1 -> x16, matrix products: 17.1 us -> 164 us  [body(): jnp.einsum('rhw,rkw->rhk', shard, request_keys, preferred_element_type=jn...]
    ppermute x0 -> x15, starting transfers between devices: none -> 32 us  [the longest x7 31.4 us: ring_apply(): lax.ppermute(from_right, axis, backward)]
    ppermute x0 -> x15, waiting for transfers between devices: none -> 26.6 us  [the longest x8 22.7 us: ring_apply(): next_left = lax.ppermute(from_left, axis, ahead) if hop < middle else None]
    all_gather x1 -> x0, waiting for transfers between devices: 22.8 us -> none  [body(): lax.all_gather(queries, 'seq', axis=1, tiled=True)]
    gather x0 -> x1, local copies, waits for them, and re-layouts: none -> 9.19 us  [ring_apply(): tiles = tiles[(jnp.arange(size) - index + middle) % size]]
    reduce_max x0 -> x1, other arithmetic: none -> 5.78 us  [body(): highest = lax.pmax(jnp.max(scores, axis=2), 'seq')]
    unnamed x11 -> x23, local copies, waits for them, and re-layouts: 17.6 us -> 17.5 us
  transfers between devices with their start and end apart: 2 -> 16, of which waited for: 2 -> 6; matrix products, arithmetic and copies ran while one was open for 18% -> 44% of each run, Pallas kernels for 0% -> 0%
where the time goes in v1:
time: 470 us; the launch traced here: 469 us
  matrix products  181 us (39%)
  blocking collectives  118 us (25%)
  waiting for transfers between devices  56.5 us (12%)
  local copies, waits for them, and re-layouts  46 us (10%)
  starting transfers between devices  32 us (7%)
  other arithmetic  21.3 us (5%)
  between operations  14.3 us (3%)
    dot_general x16, matrix products, body(): jnp.einsum('rhw,rkw->rhk', shard, request_keys, preferred_element_type=jn...  164 us
    unnamed x1, blocking collectives  60.5 us
    pmax x1, blocking collectives, body(): highest = lax.pmax(jnp.max(scores, axis=2), 'seq')  57.7 us
    ppermute x7, starting transfers between devices, ring_apply(): lax.ppermute(from_right, axis, backward)  31.4 us
    reduce_scatter x1, waiting for transfers between devices, body(): lax.psum_scatter(weighted, 'seq', scatter_dimension=1, tiled=True)  29.9 us
    ppermute x8, waiting for transfers between devices, ring_apply(): next_left = lax.ppermute(from_left, axis, ahead) if hop < middle else None  22.7 us
    unnamed x23, local copies, waits for them, and re-layouts  17.5 us
    dot_general x1, matrix products, body(): jnp.einsum('rhk,rkl->rhl', rounded, request_keys[:, :, :LAT], preferred_e...  16.7 us
  transfers between devices with their start and end apart: 16, of which 6 were waited for; matrix products, arithmetic and copies ran while one was open for 44% of the time, Pallas kernels for 0%

profile of v1, /device:TPU:0, one launch (start us, length us, event | category | flops | bytes accessed | tf_op | source)
XLA Modules:
  0.0 469.2 jit_solution(13442594169713378230)
XLA Ops:
  6.5 0.5 collective-permute-start
  7.0 9.9 %collective-permute-done = bf16[32,8,576]{2,1,0:T(8,128)(2,1)S(1)} collective-permute-done((bf16[32,8,576]{2,1,0:T(8,128)(2,1)}, bf16[32,8,576]{2,1,0:T(8,128)(2,1)S(1)}, u32[]{:S(2)}, u32[]{:S(2)}) %collective-permute-start) | collective-permute-done | bytes 294944 | tf_op jit(solution)/shard_map/ppermute | solution.py:24
  17.0 0.0 collective-permute-start.1
  17.0 4.4 collective-permute-start.8
  21.4 5.0 %collective-permute-done.1 = bf16[32,8,576]{2,1,0:T(8,128)(2,1)} collective-permute-done((bf16[32,8,576]{2,1,0:T(8,128)(2,1)S(1)}, bf16[32,8,576]{2,1,0:T(8,128)(2,1)}, u32[]{:S(2)}, u32[]{:S(2)}) %collective-permute-start.1) | collective-permute-done | bytes 294944 | tf_op jit(solution)/shard_map/ppermute | solution.py:24
  26.4 0.9 compare_reduce_fusion
  27.3 0.0 collective-permute-done.8
  27.3 4.5 collective-permute-start.9
  31.8 4.2 collective-permute-done.2
  36.0 1.6 sort.17
  37.6 0.0 collective-permute-done.9
  37.6 4.4 collective-permute-start.10
  42.1 3.5 collective-permute-done.3
  45.6 0.0 collective-permute-start.4
  45.6 0.7 compare_select_fusion.1
  46.3 2.4 gather_fusion
  48.7 2.9 copy.27
  51.6 8.0 %gather_fusion.1 = bf16[32,512,576]{1,2,0:T(8,128)(2,1)} fusion(bf16[4,512,576]{1,2,0:T(8,128)(2,1)S(1)} %copy.27, s32[1024]{0:T(1024)S(1)} %get-tuple-element.7), kind=kCustom, calls=%fused_computation.1 | custom fusion | bytes 37748864 | tf_op jit(solution)/shard_map/gather | solution.py:47
  59.6 4.4 collective-permute-start.11
  64.0 0.0 collective-permute-start.5
  64.0 16.9 %constant_dynamic-update-slice_fusion.1 = bf16[32,640,576]{1,2,0:T(8,128)(2,1)} fusion(bf16[32,512,576]{1,2,0:T(8,128)(2,1)} %gather_fusion.1), kind=kLoop, calls=%fused_computation.52 | loop fusion | bytes 37748736
  80.9 0.0 collective-permute-done.11
  80.9 4.5 collective-permute-start.12
  85.4 0.0 collective-permute-done.5
  85.4 0.0 collective-permute-start.6
  85.4 0.1 broadcast_compare_fusion
  85.5 0.6 concatenate.6
  86.1 3.9 collective-permute-done.12
  90.0 4.7 %collective-permute-start.13 = (bf16[32,8,576]{2,1,0:T(8,128)(2,1)S(1)}, bf16[32,8,576]{2,1,0:T(8,128)(2,1)}, u32[]{:S(2)}, u32[]{:S(2)}) collective-permute-start(bf16[32,8,576]{2,1,0:T(8,128)(2,1)S(1)} %collective-permute-done.12), channel_id=1, source_target_pairs={{0,15},{1,0},{2,1},{3,2},{4,3},{5,4},{6,5},{7,6},{8,7},{9,8},{10,9... | collective-permute-start | bytes 884744 | tf_op jit(solution)/shard_map/ppermute | solution.py:25
  94.7 0.0 collective-permute-done.6
  94.7 0.6 pad_clamp_fusion
  95.3 5.0 %constant_dynamic-update-slice_fusion = bf16[32,640,576]{1,2,0:T(8,128)(2,1)} fusion(bf16[32,640,576]{1,2,0:T(8,128)(2,1)} %constant_dynamic-update-slice_fusion.1, bf16[32,128,576]{1,2,0:T(8,128)(2,1)} %param.10), kind=kLoop, calls=%fused_computation.51 | loop fusion | bytes 9437184 | tf_op jit(solution)/shard_map/concatenate | solution.py:47
  100.3 4.4 collective-permute-start.14
  104.7 10.2 %fusion.26 = f32[16,32,8,640]{3,2,1,0:T(8,128)} fusion(bf16[32,640,576]{1,2,0:T(8,128)(2,1)} %constant_dynamic-update-slice_fusion, bf16[32,8,576]{2,1,0:T(8,128)(2,1)S(1)} %collective-permute-done.7), kind=kOutput, calls=%fused_computation.48 | convolution fusion | flops 188743680 | bytes 24543232 | tf_op jit(solution)/shard_map/rhw,rkw->rhk/dot_general | solution.py:58
  115.0 10.2 %fusion.25 = f32[16,32,8,640]{3,2,1,0:T(8,128)} fusion(f32[16,32,8,640]{3,2,1,0:T(8,128)} %fusion.26, bf16[32,640,576]{1,2,0:T(8,128)(2,1)} %constant_dynamic-update-slice_fusion, bf16[32,8,576]{2,1,0:T(8,128)(2,1)S(1)} %collective-permute-done.6), kind=kOutput, calls=%fused_computation.46 | convolution fusion | flops 188743680 | bytes 24543232 | tf_op jit(solution)/shard_map/rhw,rkw->rhk/dot_general | solution.py:58
  125.2 10.3 %fusion.24 = f32[16,32,8,640]{3,2,1,0:T(8,128)} fusion(f32[16,32,8,640]{3,2,1,0:T(8,128)} %fusion.25, bf16[32,640,576]{1,2,0:T(8,128)(2,1)} %constant_dynamic-update-slice_fusion, bf16[32,8,576]{2,1,0:T(8,128)(2,1)S(1)} %collective-permute-done.5), kind=kOutput, calls=%fused_computation.44 | convolution fusion | flops 188743680 | bytes 24543232 | tf_op jit(solution)/shard_map/rhw,rkw->rhk/dot_general | solution.py:58
  135.5 10.3 %fusion.23 = f32[16,32,8,640]{3,2,1,0:T(8,128)} fusion(f32[16,32,8,640]{3,2,1,0:T(8,128)} %fusion.24, bf16[32,640,576]{1,2,0:T(8,128)(2,1)} %constant_dynamic-update-slice_fusion, bf16[32,8,576]{2,1,0:T(8,128)(2,1)} %collective-permute-done.4), kind=kOutput, calls=%fused_computation.42 | convolution fusion | flops 188743680 | bytes 24576000 | tf_op jit(solution)/shard_map/rhw,rkw->rhk/dot_general | solution.py:58
  145.7 10.3 %fusion.22 = f32[16,32,8,640]{3,2,1,0:T(8,128)} fusion(f32[16,32,8,640]{3,2,1,0:T(8,128)} %fusion.23, bf16[32,640,576]{1,2,0:T(8,128)(2,1)} %constant_dynamic-update-slice_fusion, bf16[32,8,576]{2,1,0:T(8,128)(2,1)} %collective-permute-done.3), kind=kOutput, calls=%fused_computation.40 | convolution fusion | flops 188743680 | bytes 24576000 | tf_op jit(solution)/shard_map/rhw,rkw->rhk/dot_general | solution.py:58
  156.0 10.3 %fusion.21 = f32[16,32,8,640]{3,2,1,0:T(8,128)} fusion(f32[16,32,8,640]{3,2,1,0:T(8,128)} %fusion.22, bf16[32,640,576]{1,2,0:T(8,128)(2,1)} %constant_dynamic-update-slice_fusion, bf16[32,8,576]{2,1,0:T(8,128)(2,1)} %collective-permute-done.2), kind=kOutput, calls=%fused_computation.38 | convolution fusion | flops 188743680 | bytes 24576000 | tf_op jit(solution)/shard_map/rhw,rkw->rhk/dot_general | solution.py:58
  166.3 10.3 %fusion.20 = f32[16,32,8,640]{3,2,1,0:T(8,128)} fusion(f32[16,32,8,640]{3,2,1,0:T(8,128)} %fusion.21, bf16[32,640,576]{1,2,0:T(8,128)(2,1)} %constant_dynamic-update-slice_fusion, bf16[32,8,576]{2,1,0:T(8,128)(2,1)} %collective-permute-done.1), kind=kOutput, calls=%fused_computation.36 | convolution fusion | flops 188743680 | bytes 24576000 | tf_op jit(solution)/shard_map/rhw,rkw->rhk/dot_general | solution.py:58
  176.6 10.3 %fusion.19 = f32[16,32,8,640]{3,2,1,0:T(8,128)} fusion(f32[16,32,8,640]{3,2,1,0:T(8,128)} %fusion.20, bf16[32,640,576]{1,2,0:T(8,128)(2,1)} %constant_dynamic-update-slice_fusion, bf16[32,8,576]{2,1,0:T(8,128)(2,1)S(1)} %collective-permute-done), kind=kOutput, calls=%fused_computation.34 | convolution fusion | flops 188743680 | bytes 24543232 | tf_op jit(solution)/shard_map/rhw,rkw->rhk/dot_general | solution.py:58
  186.8 10.2 %fusion.18 = f32[16,32,8,640]{3,2,1,0:T(8,128)} fusion(f32[16,32,8,640]{3,2,1,0:T(8,128)} %fusion.19, bf16[32,640,576]{1,2,0:T(8,128)(2,1)} %constant_dynamic-update-slice_fusion, bf16[32,8,576]{2,1,0:T(8,128)(2,1)S(1)} %copy-done.2), kind=kOutput, calls=%fused_computation.32 | convolution fusion | flops 188743680 | bytes 24543232 | tf_op jit(solution)/shard_map/rhw,rkw->rhk/dot_general | solution.py:58
  197.0 10.2 %fusion.17 = f32[16,32,8,640]{3,2,1,0:T(8,128)} fusion(f32[16,32,8,640]{3,2,1,0:T(8,128)} %fusion.18, bf16[32,640,576]{1,2,0:T(8,128)(2,1)} %constant_dynamic-update-slice_fusion, bf16[32,8,576]{2,1,0:T(8,128)(2,1)S(1)} %collective-permute-done.8), kind=kOutput, calls=%fused_computation.30 | convolution fusion | flops 188743680 | bytes 24543232 | tf_op jit(solution)/shard_map/rhw,rkw->rhk/dot_general | solution.py:58
  207.3 10.3 %fusion.16 = f32[16,32,8,640]{3,2,1,0:T(8,128)} fusion(f32[16,32,8,640]{3,2,1,0:T(8,128)} %fusion.17, bf16[32,640,576]{1,2,0:T(8,128)(2,1)} %constant_dynamic-update-slice_fusion, bf16[32,8,576]{2,1,0:T(8,128)(2,1)} %collective-permute-done.9), kind=kOutput, calls=%fused_computation.28 | convolution fusion | flops 188743680 | bytes 24576000 | tf_op jit(solution)/shard_map/rhw,rkw->rhk/dot_general | solution.py:58
  217.6 10.3 %fusion.15 = f32[16,32,8,640]{3,2,1,0:T(8,128)} fusion(f32[16,32,8,640]{3,2,1,0:T(8,128)} %fusion.16, bf16[32,640,576]{1,2,0:T(8,128)(2,1)} %constant_dynamic-update-slice_fusion, bf16[32,8,576]{2,1,0:T(8,128)(2,1)} %collective-permute-done.10), kind=kOutput, calls=%fused_computation.26 | convolution fusion | flops 188743680 | bytes 24576000 | tf_op jit(solution)/shard_map/rhw,rkw->rhk/dot_general | solution.py:58
  227.9 10.3 %fusion.14 = f32[16,32,8,640]{3,2,1,0:T(8,128)} fusion(f32[16,32,8,640]{3,2,1,0:T(8,128)} %fusion.15, bf16[32,640,576]{1,2,0:T(8,128)(2,1)} %constant_dynamic-update-slice_fusion, bf16[32,8,576]{2,1,0:T(8,128)(2,1)S(1)} %copy-done.4), kind=kOutput, calls=%fused_computation.24 | convolution fusion | flops 188743680 | bytes 24543232 | tf_op jit(solution)/shard_map/rhw,rkw->rhk/dot_general | solution.py:58
  238.2 10.2 %fusion.13 = f32[16,32,8,640]{3,2,1,0:T(8,128)} fusion(f32[16,32,8,640]{3,2,1,0:T(8,128)} %fusion.14, bf16[32,640,576]{1,2,0:T(8,128)(2,1)} %constant_dynamic-update-slice_fusion, bf16[32,8,576]{2,1,0:T(8,128)(2,1)S(1)} %copy-done.6), kind=kOutput, calls=%fused_computation.22 | convolution fusion | flops 188743680 | bytes 24543232 | tf_op jit(solution)/shard_map/rhw,rkw->rhk/dot_general | solution.py:58
  248.4 10.3 %fusion.12 = f32[16,32,8,640]{3,2,1,0:T(8,128)} fusion(f32[16,32,8,640]{3,2,1,0:T(8,128)} %fusion.13, bf16[32,640,576]{1,2,0:T(8,128)(2,1)} %constant_dynamic-update-slice_fusion, bf16[32,8,576]{2,1,0:T(8,128)(2,1)} %collective-permute-done.13), kind=kOutput, calls=%fused_computation.20 | convolution fusion | flops 188743680 | bytes 24576000 | tf_op jit(solution)/shard_map/rhw,rkw->rhk/dot_general | solution.py:58
  258.7 10.3 %fusion.11 = f32[16,32,8,640]{3,2,1,0:T(8,128)} fusion(f32[16,32,8,640]{3,2,1,0:T(8,128)} %fusion.12, bf16[32,640,576]{1,2,0:T(8,128)(2,1)} %constant_dynamic-update-slice_fusion, bf16[32,8,576]{2,1,0:T(8,128)(2,1)} %collective-permute-done.14), kind=kOutput, calls=%fused_computation.18 | convolution fusion | flops 188743680 | bytes 24576000 | tf_op jit(solution)/shard_map/rhw,rkw->rhk/dot_general | solution.py:58
  268.9 9.2 %gather_fusion.2 = f32[16,32,8,640]{3,2,1,0:T(8,128)} fusion(f32[16,32,8,640]{3,2,1,0:T(8,128)} %fusion.11, s32[1024]{0:T(1024)} %pad_clamp_fusion), kind=kCustom, calls=%fused_computation.2 | custom fusion | bytes 20971584 | tf_op jit(solution)/shard_map/gather | solution.py:31
  278.1 5.8 %bitcast_reduce_fusion = f32[32,16,8]{2,0,1:T(8,128)S(1)} fusion(f32[16,32,8,640]{3,2,1,0:T(8,128)} %gather_fusion.2, pred[32,640]{1,0:T(8,128)(4,1)S(1)} %copy-done.7), kind=kLoop, calls=%fused_computation.6 | loop fusion | flops 7860224 | bytes 10522624 | tf_op jit(solution)/shard_map/reduce_max | solution.py:66
  283.9 0.1 copy.29
  284.0 57.7 %pmax.7 = f32[32,128]{0,1:T(8,128)S(1)} all-reduce(f32[32,128]{0,1:T(8,128)S(1)} %bitcast.157), channel_id=1, replica_groups=mesh['groups'=2,'seq'=16] {'seq'}, use_global_device_ids=true, to_apply=%region_4.5 | all-reduce | flops 4096 | bytes 32768 | tf_op jit(solution)/shard_map/pmax | solution.py:66
  341.7 0.1 copy.30
  341.8 16.7 %fusion = f32[32,128,512]{2,1,0:T(8,128)} fusion(bf16[32,640,576]{1,2,0:T(8,128)(2,1)} %constant_dynamic-update-slice_fusion, f32[32,128]{1,0:T(8,128)S(1)} %copy.30, pred[32,640]{1,0:T(8,128)(4,1)S(1)} %copy-done.7, f32[16,32,8,640]{3,2,1,0:T(8,128)} %gather_fusion.2), kind=kOutput, calls=%fused_computation.3 | convolution fusion | flops 2694840320 | bytes 39882752 | tf_op jit(solution)/shard_map/rhk,rkl->rhl/dot_general | solution.py:70
  358.5 0.0 reduce-scatter.2.cloned.1.call-update
  358.5 0.6 dynamic-slice
  359.9 0.1 copy.32
  360.1 9.8 %fusion.3 = f32[32,16,8]{2,0,1:T(8,128)S(1)} fusion(f32[16,32,8,640]{3,2,1,0:T(8,128)} %gather_fusion.2, f32[32,16,8]{2,0,1:T(8,128)S(1)} %copy.32, pred[32,640]{1,0:T(8,128)(4,1)S(1)} %copy-done.7), kind=kLoop, calls=%fused_computation.8 | loop fusion | flops 10481664 | bytes 10539008 | tf_op jit(solution)/shard_map/reduce_sum | solution.py:68
  369.9 0.1 copy.33
  370.0 60.5 %all-reduce.1 = f32[32,128]{0,1:T(8,128)S(1)} all-reduce(f32[32,128]{0,1:T(8,128)S(1)} %bitcast.158), channel_id=3, replica_groups=mesh['groups'=2,'seq'=16] {'seq'}, use_global_device_ids=true, to_apply=%region_7.8.clone | all-reduce | flops 4096 | bytes 32768
  430.5 0.1 copy.34
  430.6 29.9 %reduce-scatter.2.cloned.1.call-done = f32[32,8,512]{2,1,0:T(8,128)} async-done(((f32[32,128,512]{2,1,0:T(8,128)}), f32[32,8,512]{2,1,0:T(8,128)}) %reduce-scatter.2.cloned.1.call-update) | async-done | bytes 524304 | tf_op jit(solution)/shard_map/reduce_scatter | solution.py:75
  460.5 1.9 divide_convert_fusion
  (37 shorter events, 0.1 us)
Async XLA Ops:
  6.5 39.8 %copy-start = (bf16[32,64,576]{2,1,0:T(8,128)(2,1)S(1)}, bf16[32,64,576]{2,1,0:T(8,128)(2,1)}, u32[]{:S(2)}) copy-start(bf16[32,64,576]{2,1,0:T(8,128)(2,1)} %param.7) | copy-start | bytes 7077892
  6.5 454.0 %reduce-scatter.2.cloned.1.call-start = ((), (), s32[]{:S(2)}) async-start(), calls=%async_computation.1 | async-start | bytes 8912896 | tf_op jit(solution)/shard_map/reduce_scatter | solution.py:75
  6.5 10.4 %collective-permute-start = (bf16[32,8,576]{2,1,0:T(8,128)(2,1)}, bf16[32,8,576]{2,1,0:T(8,128)(2,1)S(1)}, u32[]{:S(2)}, u32[]{:S(2)}) collective-permute-start(bf16[32,8,576]{2,1,0:T(8,128)(2,1)} %param.6), channel_id=1, source_target_pairs={{0,1},{1,2},{2,3},{3,4},{4,5},{5,6},{6,7},{7,8},{8,9},{9,10},{10,1... | collective-permute-start | bytes 884744 | tf_op jit(solution)/shard_map/ppermute | solution.py:24
  17.0 9.4 %collective-permute-start.1 = (bf16[32,8,576]{2,1,0:T(8,128)(2,1)S(1)}, bf16[32,8,576]{2,1,0:T(8,128)(2,1)}, u32[]{:S(2)}, u32[]{:S(2)}) collective-permute-start(bf16[32,8,576]{2,1,0:T(8,128)(2,1)S(1)} %collective-permute-done), channel_id=1, source_target_pairs={{0,1},{1,2},{2,3},{3,4},{4,5},{5,6},{6,7},{7,8},{8,9},{9,10},{10,1... | collective-permute-start | bytes 884744 | tf_op jit(solution)/shard_map/ppermute | solution.py:24
  17.0 10.3 %collective-permute-start.8 = (bf16[32,8,576]{2,1,0:T(8,128)(2,1)}, bf16[32,8,576]{2,1,0:T(8,128)(2,1)S(1)}, u32[]{:S(2)}, u32[]{:S(2)}) collective-permute-start(bf16[32,8,576]{2,1,0:T(8,128)(2,1)} %param.6), channel_id=1, source_target_pairs={{0,15},{1,0},{2,1},{3,2},{4,3},{5,4},{6,5},{7,6},{8,7},{9,8},{10,9... | collective-permute-start | bytes 884744 | tf_op jit(solution)/shard_map/ppermute | solution.py:25
  26.4 9.6 %collective-permute-start.2 = (bf16[32,8,576]{2,1,0:T(8,128)(2,1)}, bf16[32,8,576]{2,1,0:T(8,128)(2,1)}, u32[]{:S(2)}, u32[]{:S(2)}) collective-permute-start(bf16[32,8,576]{2,1,0:T(8,128)(2,1)} %collective-permute-done.1), channel_id=1, source_target_pairs={{0,1},{1,2},{2,3},{3,4},{4,5},{5,6},{6,7},{7,8},{8,9},{9,10},{10,1... | collective-permute-start | bytes 884744 | tf_op jit(solution)/shard_map/ppermute | solution.py:24
  27.3 10.3 %collective-permute-start.9 = (bf16[32,8,576]{2,1,0:T(8,128)(2,1)S(1)}, bf16[32,8,576]{2,1,0:T(8,128)(2,1)}, u32[]{:S(2)}, u32[]{:S(2)}) collective-permute-start(bf16[32,8,576]{2,1,0:T(8,128)(2,1)S(1)} %collective-permute-done.8), channel_id=1, source_target_pairs={{0,15},{1,0},{2,1},{3,2},{4,3},{5,4},{6,5},{7,6},{8,7},{9,8},{10,9... | collective-permute-start | bytes 884744 | tf_op jit(solution)/shard_map/ppermute | solution.py:25
  36.0 9.6 %collective-permute-start.3 = (bf16[32,8,576]{2,1,0:T(8,128)(2,1)}, bf16[32,8,576]{2,1,0:T(8,128)(2,1)}, u32[]{:S(2)}, u32[]{:S(2)}) collective-permute-start(bf16[32,8,576]{2,1,0:T(8,128)(2,1)} %collective-permute-done.2), channel_id=1, source_target_pairs={{0,1},{1,2},{2,3},{3,4},{4,5},{5,6},{6,7},{7,8},{8,9},{9,10},{10,1... | collective-permute-start | bytes 884744 | tf_op jit(solution)/shard_map/ppermute | solution.py:24
  37.6 21.9 %collective-permute-start.10 = (bf16[32,8,576]{2,1,0:T(8,128)(2,1)}, bf16[32,8,576]{2,1,0:T(8,128)(2,1)}, u32[]{:S(2)}, u32[]{:S(2)}) collective-permute-start(bf16[32,8,576]{2,1,0:T(8,128)(2,1)} %collective-permute-done.9), channel_id=1, source_target_pairs={{0,15},{1,0},{2,1},{3,2},{4,3},{5,4},{6,5},{7,6},{8,7},{9,8},{10,9... | collective-permute-start | bytes 884744 | tf_op jit(solution)/shard_map/ppermute | solution.py:25
  45.6 18.4 %collective-permute-start.4 = (bf16[32,8,576]{2,1,0:T(8,128)(2,1)}, bf16[32,8,576]{2,1,0:T(8,128)(2,1)}, u32[]{:S(2)}, u32[]{:S(2)}) collective-permute-start(bf16[32,8,576]{2,1,0:T(8,128)(2,1)} %collective-permute-done.3), channel_id=1, source_target_pairs={{0,1},{1,2},{2,3},{3,4},{4,5},{5,6},{6,7},{7,8},{8,9},{9,10},{10,1... | collective-permute-start | bytes 884744 | tf_op jit(solution)/shard_map/ppermute | solution.py:24
  59.6 25.8 %copy-start.8 = (s32[32]{0:T(128)S(1)}, s32[32]{0:T(128)}, u32[]{:S(2)}) copy-start(s32[32]{0:T(128)} %param.11) | copy-start | bytes 388
  59.6 21.3 %collective-permute-start.11 = (bf16[32,8,576]{2,1,0:T(8,128)(2,1)}, bf16[32,8,576]{2,1,0:T(8,128)(2,1)S(1)}, u32[]{:S(2)}, u32[]{:S(2)}) collective-permute-start(bf16[32,8,576]{2,1,0:T(8,128)(2,1)} %collective-permute-done.10), channel_id=1, source_target_pairs={{0,15},{1,0},{2,1},{3,2},{4,3},{5,4},{6,5},{7,6},{8,7},{9,8},{10,9... | collective-permute-start | bytes 884744 | tf_op jit(solution)/shard_map/ppermute | solution.py:25
  64.0 21.4 %collective-permute-start.5 = (bf16[32,8,576]{2,1,0:T(8,128)(2,1)}, bf16[32,8,576]{2,1,0:T(8,128)(2,1)S(1)}, u32[]{:S(2)}, u32[]{:S(2)}) collective-permute-start(bf16[32,8,576]{2,1,0:T(8,128)(2,1)} %collective-permute-done.4), channel_id=1, source_target_pairs={{0,1},{1,2},{2,3},{3,4},{4,5},{5,6},{6,7},{7,8},{8,9},{9,10},{10,1... | collective-permute-start | bytes 884744 | tf_op jit(solution)/shard_map/ppermute | solution.py:24
  80.9 34.1 %copy-start.3 = (bf16[32,8,576]{2,1,0:T(8,128)(2,1)}, bf16[32,8,576]{2,1,0:T(8,128)(2,1)S(1)}, u32[]{:S(2)}) copy-start(bf16[32,8,576]{2,1,0:T(8,128)(2,1)S(1)} %collective-permute-done.11) | copy-start | bytes 884740
  80.9 9.1 %collective-permute-start.12 = (bf16[32,8,576]{2,1,0:T(8,128)(2,1)S(1)}, bf16[32,8,576]{2,1,0:T(8,128)(2,1)S(1)}, u32[]{:S(2)}, u32[]{:S(2)}) collective-permute-start(bf16[32,8,576]{2,1,0:T(8,128)(2,1)S(1)} %collective-permute-done.11), channel_id=1, source_target_pairs={{0,15},{1,0},{2,1},{3,2},{4,3},{5,4},{6,5},{7,6},{8,7},{9,8},{10,9... | collective-permute-start | bytes 884744 | tf_op jit(solution)/shard_map/ppermute | solution.py:25
  85.4 9.3 %collective-permute-start.6 = (bf16[32,8,576]{2,1,0:T(8,128)(2,1)S(1)}, bf16[32,8,576]{2,1,0:T(8,128)(2,1)S(1)}, u32[]{:S(2)}, u32[]{:S(2)}) collective-permute-start(bf16[32,8,576]{2,1,0:T(8,128)(2,1)S(1)} %collective-permute-done.5), channel_id=1, source_target_pairs={{0,1},{1,2},{2,3},{3,4},{4,5},{5,6},{6,7},{7,8},{8,9},{9,10},{10,1... | collective-permute-start | bytes 884744 | tf_op jit(solution)/shard_map/ppermute | solution.py:24
  90.0 25.0 %copy-start.5 = (bf16[32,8,576]{2,1,0:T(8,128)(2,1)}, bf16[32,8,576]{2,1,0:T(8,128)(2,1)S(1)}, u32[]{:S(2)}) copy-start(bf16[32,8,576]{2,1,0:T(8,128)(2,1)S(1)} %collective-permute-done.12) | copy-start | bytes 884740
  90.0 10.3 %collective-permute-start.13 = (bf16[32,8,576]{2,1,0:T(8,128)(2,1)S(1)}, bf16[32,8,576]{2,1,0:T(8,128)(2,1)}, u32[]{:S(2)}, u32[]{:S(2)}) collective-permute-start(bf16[32,8,576]{2,1,0:T(8,128)(2,1)S(1)} %collective-permute-done.12), channel_id=1, source_target_pairs={{0,15},{1,0},{2,1},{3,2},{4,3},{5,4},{6,5},{7,6},{8,7},{9,8},{10,9... | collective-permute-start | bytes 884744 | tf_op jit(solution)/shard_map/ppermute | solution.py:25
  94.7 10.0 %collective-permute-start.7 = (bf16[32,8,576]{2,1,0:T(8,128)(2,1)S(1)}, bf16[32,8,576]{2,1,0:T(8,128)(2,1)S(1)}, u32[]{:S(2)}, u32[]{:S(2)}) collective-permute-start(bf16[32,8,576]{2,1,0:T(8,128)(2,1)S(1)} %collective-permute-done.6), channel_id=1, source_target_pairs={{0,1},{1,2},{2,3},{3,4},{4,5},{5,6},{6,7},{7,8},{8,9},{9,10},{10,1... | collective-permute-start | bytes 884744 | tf_op jit(solution)/shard_map/ppermute | solution.py:24
  100.3 158.4 %collective-permute-start.14 = (bf16[32,8,576]{2,1,0:T(8,128)(2,1)}, bf16[32,8,576]{2,1,0:T(8,128)(2,1)}, u32[]{:S(2)}, u32[]{:S(2)}) collective-permute-start(bf16[32,8,576]{2,1,0:T(8,128)(2,1)} %collective-permute-done.13), channel_id=1, source_target_pairs={{0,15},{1,0},{2,1},{3,2},{4,3},{5,4},{6,5},{7,6},{8,7},{9,8},{10,9... | collective-permute-start | bytes 884744 | tf_op jit(solution)/shard_map/ppermute | solution.py:25
  176.6 10.3 %copy-start.2 = (bf16[32,8,576]{2,1,0:T(8,128)(2,1)S(1)}, bf16[32,8,576]{2,1,0:T(8,128)(2,1)}, u32[]{:S(2)}) copy-start(bf16[32,8,576]{2,1,0:T(8,128)(2,1)} %param.6) | copy-start | bytes 884740
  217.5 10.3 %copy-start.4 = (bf16[32,8,576]{2,1,0:T(8,128)(2,1)S(1)}, bf16[32,8,576]{2,1,0:T(8,128)(2,1)}, u32[]{:S(2)}) copy-start(bf16[32,8,576]{2,1,0:T(8,128)(2,1)} %copy-done.3) | copy-start | bytes 884740
  227.9 10.3 %copy-start.6 = (bf16[32,8,576]{2,1,0:T(8,128)(2,1)S(1)}, bf16[32,8,576]{2,1,0:T(8,128)(2,1)}, u32[]{:S(2)}) copy-start(bf16[32,8,576]{2,1,0:T(8,128)(2,1)} %copy-done.5) | copy-start | bytes 884740
  268.9 9.2 %copy-start.7 = (pred[32,640]{1,0:T(8,128)(4,1)S(1)}, pred[32,640]{1,0:T(8,128)(4,1)}, u32[]{:S(2)}) copy-start(pred[32,640]{1,0:T(8,128)(4,1)} %concatenate.6) | copy-start | bytes 61444
  341.8 16.8 %copy-start.9 = (u32[32]{0:T(128)S(1)}, u32[32]{0:T(128)}, u32[]{:S(2)}) copy-start(u32[32]{0:T(128)} %constant.48) | copy-start | bytes 388
  358.5 103.9 %copy-start.1 = (bf16[32,64,576]{2,1,0:T(8,128)(2,1)S(1)}, bf16[32,64,576]{2,1,0:T(8,128)(2,1)}, u32[]{:S(2)}) copy-start(bf16[32,64,576]{2,1,0:T(8,128)(2,1)} %param.7) | copy-start | bytes 7077892
Sparse Core Ops, SparseCore 0:
  358.6 101.8 reduce-scatter.1
